TPU v7x, 32 devices: a whole 2x2x4 slice. The times are simulated.
32 devices in a mesh: ell: 4 (over y, x), blk: 8 (over z, core).
Axes of the slice: x: 2, y: 2, z: 4, core: 2. Of those that a mesh axis runs over, the one named last changes fastest.
Arguments:
- wigner: bfloat16 [8, 17, 2101248], P(None, None, ('ell', 'blk')), may hold values from -6 to 6
- sky_alm: float32 [2, 2101248], P(None, ('ell', 'blk')), may hold values from -0.03125 to 0.03125
- beam_blm: float32 [2, 17, 2048], replicated, may hold values from -4.25 to 4.25
- slot_col: int32 [2101248], P(('ell', 'blk')), may hold values from -1 to 255, as said below
- slot_ell: int32 [2101248], P(('ell', 'blk')), may hold values from 0 to 2047, as said below
- order_of_column: int32 [2048], replicated, may hold values from 0 to 2047, as said below
Outputs:
- conv_cube: float32 [8, 32, 4096], P('ell', 'blk')
Inputs may be any that keep to these rules, and one draw needn't show every extreme that they name: `slot_col`: slot block b (slots b * 65664 to b * 65664 + 65663) belongs to ell index b // 8 and blk index b % 8; at most 65568 slots of a block are live, and some blocks have exactly that many. `slot_ell`: every pair (l, m) with m <= l < 2048 stands in exactly one live slot; within a blk group, higher ell indices hold degrees no lower than those of lower ell indices. `order_of_column`: A permutation of 0 to 2047; every blk group's orders hold the same number of pairs.
All inputs are finite; a program needn't handle non-finite values.
Results may differ from a plain program's by a relative error of at most 0.0029.
Values sent between devices are 32-bit elements; how exact they have to be, the bound alone decides.
A program may use at most 256 MiB of HBM per device.

v0:
```python
import functools
import math

import jax
import jax.numpy as jnp
from jax import lax
from jax.experimental import pallas as pl
from jax.experimental.pallas import tpu as pltpu
from jax.sharding import PartitionSpec as P

NPSI = 32
LANES = 128
SUBLANES = 8


def phase_table(rows, cols, period):
    product = (
        jnp.arange(rows, dtype=jnp.int32)[:, None]
        * jnp.arange(cols, dtype=jnp.int32)[None, :]
        % period
    )
    angle = product.astype(jnp.float32) * (2.0 * math.pi / period)
    return (jnp.cos(angle), jnp.sin(angle))


def psi_table(order_count, samples):
    cosines, sine_terms = phase_table(order_count, samples, samples)
    real_row = jnp.stack([cosines, sine_terms], axis=1)
    imag_row = jnp.stack([-sine_terms, cosines], axis=1)
    return jnp.stack([real_row, imag_row], axis=0)


def to_phi(fields, order_of_column):
    cycles = fields.shape[0]
    samples = fields.shape[2]
    degrees = fields.shape[3]
    period = 2 * degrees
    inner = 2 ** ((period.bit_length() - 1) // 2)
    outer = period // inner
    highest = lax.Precision.HIGH
    high_part = order_of_column // inner
    low_part = order_of_column % inner
    turns = high_part[:, None] * jnp.arange(outer, dtype=jnp.int32)[None, :] % outer
    angle = turns.astype(jnp.float32) * (2.0 * math.pi / outer)
    cos_first = jnp.cos(angle)
    sin_first = jnp.sin(angle)
    select = (low_part[:, None] == jnp.arange(inner, dtype=jnp.int32)[None, :]).astype(jnp.float32)
    real_in = fields[:, 0]
    imag_in = fields[:, 1]
    weighted_re = real_in[..., None] * cos_first - imag_in[..., None] * sin_first
    weighted_im = real_in[..., None] * sin_first + imag_in[..., None] * cos_first
    first_re = jnp.einsum("tpcj,cv->tpvj", weighted_re, select, precision=highest)
    first_im = jnp.einsum("tpcj,cv->tpvj", weighted_im, select, precision=highest)
    cos_twist, sin_twist = phase_table(inner, outer, period)
    twist_re = first_re * cos_twist - first_im * sin_twist
    twist_im = first_re * sin_twist + first_im * cos_twist
    cos_last, sin_last = phase_table(inner, inner, inner)
    result = jnp.einsum("tpvj,vw->tpwj", twist_re, cos_last, precision=highest) - jnp.einsum(
        "tpvj,vw->tpwj", twist_im, sin_last, precision=highest
    )
    return result.reshape(cycles, samples, period)


def largest_part(total, most):
    return max(part for part in range(1, total + 1) if total % part == 0 and part <= most)


def beam_table(beam):
    orders, degrees = beam.shape[1], beam.shape[2]
    whole = orders // SUBLANES * SUBLANES
    rest = orders - whole
    rows = [beam[0, :whole], beam[1, :whole]]
    if rest > 0:
        real, imag = beam[0, whole:], beam[1, whole:]
        short = SUBLANES // 4 if rest <= SUBLANES // 4 else SUBLANES
        real = jnp.pad(real, ((0, short - rest), (0, 0)))
        imag = jnp.pad(imag, ((0, short - rest), (0, 0)))
        rows += [real, imag, -imag, real] if short < SUBLANES else [real, imag]
    table = jnp.concatenate(rows, axis=0)
    tiles = degrees // LANES
    return table.reshape(table.shape[0], tiles, LANES).transpose(1, 0, 2)


def lane_pick(table, index):
    return lax.gather(
        table,
        index[..., None],
        lax.GatherDimensionNumbers(
            offset_dims=(),
            collapsed_slice_dims=(1,),
            start_index_map=(1,),
            operand_batching_dims=(0,),
            start_indices_batching_dims=(0,),
        ),
        slice_sizes=(1, 1),
        mode=lax.GatherScatterMode.PROMISE_IN_BOUNDS,
    )


def sums_kernel(
    orders, sub, wig_ref, sky_ref, col_ref, ell_ref, table_ref, out_ref, *scratch
):
    cycles = wig_ref.shape[1]
    chunk = wig_ref.shape[2]
    tiles, rows, _ = table_ref.shape
    groups = rows // SUBLANES
    whole = orders // SUBLANES
    rest = orders - whole * SUBLANES
    packed = 0 < rest <= SUBLANES // 4
    coeff_refs, value_refs, hot_refs = scratch[0:2], scratch[2:4], scratch[4:6]
    cols = out_ref.shape[1]
    parts = sub // LANES

    live = col_ref[...] >= 0
    degree = ell_ref[...]
    top = jnp.max(jnp.where(live, degree, 0).astype(jnp.float32)).astype(jnp.int32) // LANES
    low = jnp.min(jnp.where(live, degree, tiles * LANES - 1).astype(jnp.float32)).astype(jnp.int32) // LANES
    span = top - low + 1

    def pick_all(count, first, start, coeff_ref):
        for part in range(parts):
            lanes = pl.ds(pl.multiple_of(start + part * LANES, LANES), LANES)
            ell = jnp.broadcast_to(ell_ref[:, lanes], (SUBLANES, LANES))
            high = (ell >> 7) - first
            index = ell & (LANES - 1)
            picked = [jnp.zeros((SUBLANES, LANES), jnp.float32) for _ in range(groups)]
            for tile in range(count):
                here = high == tile
                for group in range(groups):
                    entry = table_ref[first + tile, pl.ds(group * SUBLANES, SUBLANES), :]
                    picked[group] = jnp.where(here, lane_pick(entry, index), picked[group])
            sky_re = jnp.broadcast_to(sky_ref[0:1, lanes], (SUBLANES, LANES))
            sky_im = jnp.broadcast_to(sky_ref[1:2, lanes], (SUBLANES, LANES))
            out = []
            for group in range(whole):
                out.append(sky_re * picked[group] - sky_im * picked[whole + group])
            for group in range(whole):
                out.append(sky_re * picked[whole + group] + sky_im * picked[group])
            if packed:
                row = lax.broadcasted_iota(jnp.int32, (SUBLANES, LANES), 0)
                term = picked[2 * whole] * jnp.where(row < SUBLANES // 2, sky_re, sky_im)
                out.append(term + pltpu.roll(term, SUBLANES // 2, 0))
            elif rest > 0:
                out.append(sky_re * picked[2 * whole] - sky_im * picked[2 * whole + 1])
                out.append(sky_re * picked[2 * whole + 1] + sky_im * picked[2 * whole])
            here = slice(part * LANES, (part + 1) * LANES)
            for group, block in enumerate(out):
                coeff_ref[pl.ds(group * SUBLANES, SUBLANES), here] = block

    def row_of(part, order):
        if order < whole * SUBLANES:
            return part * whole * SUBLANES + order
        step = SUBLANES // 4 if packed else SUBLANES
        return 2 * whole * SUBLANES + part * step + order - whole * SUBLANES

    def run(count, first):
        halves = chunk // sub

        def products(half, which):
            start = pl.multiple_of(half * sub, LANES)
            coeff, value, hot = coeff_refs[which], value_refs[which], hot_refs[which]
            pick_all(count, first, start, coeff)
            lanes = pl.ds(start, sub)
            for order in range(orders):
                wig = wig_ref[order, :, lanes].astype(jnp.float32)
                real = wig * coeff[pl.ds(row_of(0, order), 1), :]
                imag = wig * coeff[pl.ds(row_of(1, order), 1), :]
                both = jnp.concatenate([real, imag], axis=0).astype(jnp.bfloat16)
                value[pl.ds(order * 2 * cycles, 2 * cycles), :] = both
            col = jnp.broadcast_to(col_ref[:, lanes], (cols, sub))
            row = lax.broadcasted_iota(jnp.int32, (cols, sub), 0)
            hot[...] = (row == col).astype(jnp.float32).astype(jnp.bfloat16)

        def add_up(which):
            out_ref[...] += lax.dot_general(
                value_refs[which][...],
                hot_refs[which][...],
                (((1,), (1,)), ((), ())),
                preferred_element_type=jnp.float32,
            )

        products(0, 1)

        @pl.loop(0, (halves - 1) // 2)
        def _(pair):
            add_up(1)
            products(2 * pair + 1, 0)
            add_up(0)
            products(2 * pair + 2, 1)

        add_up(1)
        if halves % 2 == 0:
            products(halves - 1, 0)
            add_up(0)

    @pl.when(pl.program_id(0) == 0)
    def _():
        out_ref[...] = jnp.zeros_like(out_ref)

    counts = sorted({min(c, tiles) for c in (4, 9)})
    below = 0
    for count in counts:
        first = jnp.minimum(low, tiles - count)

        @pl.when((span > below) & (span <= count) if below else span <= count)
        def _():
            run(count, first)

        below = count
    if below < tiles:

        @pl.when(span > below)
        def _():
            run(tiles, 0)


def order_sums(wigner, sky_alm, beam_blm, slot_col, slot_ell, cols):
    cycles, orders, slots = wigner.shape
    tiles = slots // LANES
    chunk = LANES * largest_part(tiles, 64)
    sub = LANES * largest_part(chunk // LANES, 3)
    table = beam_table(beam_blm)
    rows = orders * 2 * cycles
    return pl.pallas_call(
        functools.partial(sums_kernel, orders, sub),
        out_shape=jax.ShapeDtypeStruct((rows, cols), jnp.float32),
        grid=(slots // chunk,),
        in_specs=[
            pl.BlockSpec((orders, cycles, chunk), lambda i: (0, 0, i)),
            pl.BlockSpec((2, chunk), lambda i: (0, i)),
            pl.BlockSpec((1, chunk), lambda i: (0, i)),
            pl.BlockSpec((1, chunk), lambda i: (0, i)),
            pl.BlockSpec(table.shape, lambda i: (0, 0, 0)),
        ],
        out_specs=pl.BlockSpec((rows, cols), lambda i: (0, 0)),
        scratch_shapes=[
            *[pltpu.VMEM((table.shape[1], sub), jnp.float32) for _ in range(2)],
            *[pltpu.VMEM((rows, sub), jnp.bfloat16) for _ in range(2)],
            *[pltpu.VMEM((cols, sub), jnp.bfloat16) for _ in range(2)],
        ],
        compiler_params=pltpu.CompilerParams(
            dimension_semantics=("arbitrary",), vmem_limit_bytes=48 * 1024 * 1024
        ),
        name="order_sums",
    )(wigner.transpose(1, 0, 2), sky_alm, slot_col[None, :], slot_ell[None, :], table)


def on_device(wigner, sky_alm, beam_blm, slot_col, slot_ell, order_of_column):
    cycle_total = wigner.shape[0]
    order_count = wigner.shape[1]
    blk_count = lax.axis_size("blk")
    col_count = order_of_column.shape[0] // blk_count
    col_sums = order_sums(wigner, sky_alm, beam_blm, slot_col, slot_ell, col_count)
    by_cycle = col_sums.reshape(order_count, 2, cycle_total, col_count).transpose(2, 1, 0, 3)
    ell_count = lax.axis_size("ell")
    partials = by_cycle.reshape((ell_count, cycle_total // ell_count) + by_cycle.shape[1:])
    summed = lax.all_to_all(partials, "ell", split_axis=0, concat_axis=0, tiled=True).sum(axis=0)
    owned = jnp.einsum(
        "trkc,rksp->tspc",
        summed,
        psi_table(order_count, NPSI),
        precision=lax.Precision.HIGHEST,
    )
    return to_phi(
        lax.all_to_all(owned, "blk", split_axis=2, concat_axis=3, tiled=True), order_of_column
    )


def solution(mesh):
    return jax.shard_map(
        on_device,
        mesh=mesh,
        in_specs=(
            P(None, None, ("ell", "blk")),
            P(None, ("ell", "blk")),
            P(),
            P(("ell", "blk")),
            P(("ell", "blk")),
            P(),
        ),
        out_specs=P("ell", "blk", None),
        check_vma=False,
    )
```

profile of v0, /device:TPU:0, one launch (start us, length us, event | category | flops | bytes accessed | tf_op | source)
XLA Modules:
  0.0 84.1 jit_solution(12360023628827284778)
XLA Ops:
  0.0 0.8 slice_bitcast_fusion.2
  0.8 1.3 %fusion.87 = (f32[1,16,2048]{2,0,1:T(1,128)S(1)}, f32[1,16,2048]{2,0,1:T(1,128)S(1)}) fusion(f32[2,17,2048]{2,0,1:T(2,128)} %param.8), kind=kLoop, calls=%fused_computation.115 | loop fusion | bytes 524288 | tf_op jit(solution)/shard_map/slice | solution.py:72
  2.3 1.1 %broadcast_in_dim.4.col_ref = s32[1,65664]{1,0:T(1,128)S(1)} reshape(s32[65664]{0:T(1024)} %param.9) | data formatting | bytes 525312 | tf_op jit(solution)/shard_map/broadcast_in_dim | solution.py:245
  3.4 1.1 %broadcast_in_dim.5.ell_ref = s32[1,65664]{1,0:T(1,128)S(1)} reshape(s32[65664]{0:T(1024)} %param.10) | data formatting | bytes 525312 | tf_op jit(solution)/shard_map/broadcast_in_dim | solution.py:245
  4.7 1.0 %copy-done = f32[2,65664]{1,0:T(2,128)S(1)} copy-done((f32[2,65664]{1,0:T(2,128)S(1)}, f32[2,65664]{1,0:T(2,128)}, u32[]{:S(2)}) %copy-start) | copy-done | bytes 525336
  5.7 47.7 %order_sums.1 = f32[272,256]{1,0:T(8,128)S(1)} custom-call(bf16[17,8,65664]{2,1,0:T(8,128)(2,1)} %bitcast.75, f32[2,65664]{1,0:T(2,128)S(1)} %copy-done, s32[1,65664]{1,0:T(1,128)S(1)} %broadcast_in_dim.4.col_ref, s32[1,65664]{1,0:T(1,128)S(1)} %broadcast_in_dim.5.ell_ref, f32[16,40,128]{2,1,0:T(8,128)S(1)} %bitcast.73), custom_call_target="tpu_custom_call" | custom-call | tf_op jit(solution)/shard_map/order_sums/pallas_call | solution.py:224
  53.4 0.1 copy.26
  53.6 0.9 %copy.27 = f32[4,2,2,17,256]{4,1,2,3,0:T(2,128)} copy(f32[4,2,2,17,256]{4,2,3,1,0:T(2,128)S(1)} %bitcast.76) | data formatting | bytes 557056 | tf_op jit(solution)/shard_map/reshape | solution.py:256
  54.4 4.9 %all-to-all-start = ((f32[4,2,2,17,256]{4,1,2,3,0:T(2,128)}), f32[4,2,2,17,256]{4,1,2,3,0:T(2,128)S(1)}, u32[]{:S(2)}, u32[]{:S(2)}) async-start(f32[4,2,2,17,256]{4,1,2,3,0:T(2,128)} %copy.27), calls=%async_computation | async-start | bytes 557056 | tf_op jit(solution)/shard_map/all_to_all | solution.py:257
  59.5 5.2 %all-to-all-done = f32[4,2,2,17,256]{4,1,2,3,0:T(2,128)S(1)} async-done(((f32[4,2,2,17,256]{4,1,2,3,0:T(2,128)}), f32[4,2,2,17,256]{4,1,2,3,0:T(2,128)S(1)}, u32[]{:S(2)}, u32[]{:S(2)}) %all-to-all-start) | async-done | bytes 278560 | tf_op jit(solution)/shard_map/all_to_all | solution.py:257
  64.7 0.1 reduce_sum.9
  64.9 0.3 convolution_bitcast_fusion
  65.2 0.8 copy.30
  65.9 5.2 %all-to-all-start.1 = ((f32[2,2,32,256]{3,0,1,2:T(2,128)}), f32[2,2,32,256]{3,0,1,2:T(2,128)S(1)}, u32[]{:S(2)}, u32[]{:S(2)}) async-start(f32[2,2,32,256]{3,0,1,2:T(2,128)} %copy.30), calls=%async_computation.1 | async-start | bytes 262144 | tf_op jit(solution)/shard_map/all_to_all | solution.py:265
  71.2 2.0 %fusion.36 = (f32[2048,64]{0,1:T(8,128)S(1)}, f32[2048,64]{0,1:T(8,128)S(1)}) fusion(s32[2048]{0:T(1024)S(1)} %get-tuple-element.14), kind=kLoop, calls=%fused_computation.40 | loop fusion | flops 1835008 | bytes 1056768 | tf_op jit(solution)/shard_map/cos | solution.py:45
  73.2 0.1 fusion.64
  73.5 0.2 fusion.63
  73.7 4.3 %all-to-all-done.1 = f32[2,2,32,256]{3,0,1,2:T(2,128)S(1)} async-done(((f32[2,2,32,256]{3,0,1,2:T(2,128)}), f32[2,2,32,256]{3,0,1,2:T(2,128)S(1)}, u32[]{:S(2)}, u32[]{:S(2)}) %all-to-all-start.1) | async-done | bytes 131104 | tf_op jit(solution)/shard_map/all_to_all | solution.py:265
  77.9 0.1 copy.45
  78.1 2.1 %fusion.4 = f32[64,2,4,64]{3,0,2,1:T(8,128)S(1)} fusion(f32[2048,64]{0,1:T(8,128)S(1)} %get-tuple-element.16, f32[2,4,2048]{2,1,0:T(4,128)S(1)} %get-tuple-element.10, f32[2048,64]{0,1:T(8,128)S(1)} %get-tuple-element.15, f32[2,4,2048]{2,1,0:T(4,128)S(1)} %get-tuple-element.9, s32[2048]{0:T(1024)S(1)} %get-tuple-element.13), kind=kOutput, calls=%fused_computation.4 | convolution fusion | flops 405929984 | bytes 1318912 | tf_op jit(solution)/shard_map/tpcj,cv->tpvj/dot_general | solution.py:52
  80.3 2.1 %fusion = f32[64,2,4,64]{3,0,2,1:T(8,128)S(1)} fusion(f32[2048,64]{0,1:T(8,128)S(1)} %get-tuple-element.16, f32[2,4,2048]{2,1,0:T(4,128)S(1)} %get-tuple-element.10, f32[2048,64]{0,1:T(8,128)S(1)} %get-tuple-element.15, f32[2,4,2048]{2,1,0:T(4,128)S(1)} %get-tuple-element.9, s32[2048]{0:T(1024)S(1)} %get-tuple-element.13), kind=kOutput, calls=%fused_computation | convolution fusion | flops 405929984 | bytes 1318912 | tf_op jit(solution)/shard_map/tpcj,cv->tpvj/dot_general | solution.py:53
  82.4 0.4 fusion.27
  82.8 0.4 fusion.16
  83.3 0.8 reshape.181
  (15 shorter events, 0.6 us)
Async XLA Ops:
  4.6 1.0 %copy-start = (f32[2,65664]{1,0:T(2,128)S(1)}, f32[2,65664]{1,0:T(2,128)}, u32[]{:S(2)}) copy-start(f32[2,65664]{1,0:T(2,128)} %sky_ref.1) | copy-start | bytes 1575940
  5.7 53.8 %copy-start.1 = (s32[2048]{0:T(1024)S(1)}, s32[2048]{0:T(1024)}, u32[]{:S(2)}) copy-start(s32[2048]{0:T(1024)} %param.11) | copy-start | bytes 24580
  54.4 10.3 %all-to-all-start = ((f32[4,2,2,17,256]{4,1,2,3,0:T(2,128)}), f32[4,2,2,17,256]{4,1,2,3,0:T(2,128)S(1)}, u32[]{:S(2)}, u32[]{:S(2)}) async-start(f32[4,2,2,17,256]{4,1,2,3,0:T(2,128)} %copy.27), calls=%async_computation | async-start | bytes 557056 | tf_op jit(solution)/shard_map/all_to_all | solution.py:257
  65.9 12.0 %all-to-all-start.1 = ((f32[2,2,32,256]{3,0,1,2:T(2,128)}), f32[2,2,32,256]{3,0,1,2:T(2,128)S(1)}, u32[]{:S(2)}, u32[]{:S(2)}) async-start(f32[2,2,32,256]{3,0,1,2:T(2,128)} %copy.30), calls=%async_computation.1 | async-start | bytes 262144 | tf_op jit(solution)/shard_map/all_to_all | solution.py:265
where the time goes:
time: 84.6 us; the launch traced here: 84.1 us
  Pallas kernels  47.7 us (56%)
  starting transfers between devices  10.1 us (12%)
  waiting for transfers between devices  9.48 us (11%)
  local copies, waits for them, and re-layouts  8.47 us (10%)
  matrix products  5.46 us (6%)
  other arithmetic  2.63 us (3%)
    pallas_call x1, Pallas kernels, order_sums(): pl.pallas_call(functools.partial(sums_kernel, orders, sub), out_shape=jax...  47.7 us
    all_to_all x1, starting transfers between devices, on_device(): lax.all_to_all(owned, 'blk', split_axis=2, concat_axis=3, tiled=True)  5.25 us
    all_to_all x1, waiting for transfers between devices, on_device(): lax.all_to_all(partials, 'ell', split_axis=0, concat_axis=0, tiled=True)  5.23 us
    all_to_all x1, starting transfers between devices, on_device(): lax.all_to_all(partials, 'ell', split_axis=0, concat_axis=0, tiled=True)  4.89 us
    all_to_all x1, waiting for transfers between devices, on_device(): lax.all_to_all(owned, 'blk', split_axis=2, concat_axis=3, tiled=True)  4.25 us
    dot_general x1, matrix products, to_phi(): jnp.einsum('tpcj,cv->tpvj', weighted_im, select, precision=highest)  2.14 us
    dot_general x1, matrix products, to_phi(): jnp.einsum('tpcj,cv->tpvj', weighted_re, select, precision=highest)  2.14 us
    cos x1, other arithmetic, to_phi(): cos_first = jnp.cos(angle)  2.04 us
  transfers between devices with their start and end apart: 2, of which 2 were waited for; matrix products, arithmetic and copies ran while one was open for 3% of the time, Pallas kernels for 0%

commit v1 on v0

v1 whole, which is shorter than its diff:
```python
import functools
import math

import jax
import jax.numpy as jnp
from jax import lax
from jax.experimental import pallas as pl
from jax.experimental.pallas import tpu as pltpu
from jax.sharding import PartitionSpec as P

NPSI = 32
LANES = 128
SUBLANES = 8
MXU = 256
MXU_ROWS = 1024
TRIP = 16


def phase_table(rows, cols, period):
    product = (
        jnp.arange(rows, dtype=jnp.int32)[:, None]
        * jnp.arange(cols, dtype=jnp.int32)[None, :]
        % period
    )
    angle = product.astype(jnp.float32) * (2.0 * math.pi / period)
    return (jnp.cos(angle), jnp.sin(angle))


def psi_table(order_count, samples):
    cosines, sine_terms = phase_table(order_count, samples, samples)
    real_row = jnp.stack([cosines, sine_terms], axis=1)
    imag_row = jnp.stack([-sine_terms, cosines], axis=1)
    return jnp.stack([real_row, imag_row], axis=0)


def to_phi(fields, order_of_column):
    cycles = fields.shape[0]
    samples = fields.shape[2]
    degrees = fields.shape[3]
    period = 2 * degrees
    inner = 2 ** ((period.bit_length() - 1) // 2)
    outer = period // inner
    highest = lax.Precision.HIGH
    high_part = order_of_column // inner
    low_part = order_of_column % inner
    turns = high_part[:, None] * jnp.arange(outer, dtype=jnp.int32)[None, :] % outer
    angle = turns.astype(jnp.float32) * (2.0 * math.pi / outer)
    cos_first = jnp.cos(angle)
    sin_first = jnp.sin(angle)
    select = (low_part[:, None] == jnp.arange(inner, dtype=jnp.int32)[None, :]).astype(jnp.float32)
    real_in = fields[:, 0]
    imag_in = fields[:, 1]
    weighted_re = real_in[..., None] * cos_first - imag_in[..., None] * sin_first
    weighted_im = real_in[..., None] * sin_first + imag_in[..., None] * cos_first
    first_re = jnp.einsum("tpcj,cv->tpvj", weighted_re, select, precision=highest)
    first_im = jnp.einsum("tpcj,cv->tpvj", weighted_im, select, precision=highest)
    cos_twist, sin_twist = phase_table(inner, outer, period)
    twist_re = first_re * cos_twist - first_im * sin_twist
    twist_im = first_re * sin_twist + first_im * cos_twist
    cos_last, sin_last = phase_table(inner, inner, inner)
    result = jnp.einsum("tpvj,vw->tpwj", twist_re, cos_last, precision=highest) - jnp.einsum(
        "tpvj,vw->tpwj", twist_im, sin_last, precision=highest
    )
    return result.reshape(cycles, samples, period)


def lane_pick(table, index):
    return lax.gather(
        table,
        index[..., None],
        lax.GatherDimensionNumbers(
            offset_dims=(),
            collapsed_slice_dims=(1,),
            start_index_map=(1,),
            operand_batching_dims=(0,),
            start_indices_batching_dims=(0,),
        ),
        slice_sizes=(1, 1),
        mode=lax.GatherScatterMode.PROMISE_IN_BOUNDS,
    )


def pick_span(col_ref, ell_ref, tiles):
    live = col_ref[...] >= 0
    degree = ell_ref[...]
    last = tiles * LANES - 1
    top = jnp.max(jnp.where(live, degree, 0).astype(jnp.float32)).astype(jnp.int32)
    low = jnp.min(jnp.where(live, degree, last).astype(jnp.float32)).astype(jnp.int32)
    return low // LANES, top // LANES


def sums_kernel(
    orders, cols, trips, wig_hbm, sky_ref, col_ref, ell_ref, beam_ref, out_ref, wig_buf, tail_buf, *scratch
):
    coeff_refs, sems, tail_sem = scratch[0:2], scratch[2], scratch[3]
    cycles = wig_hbm.shape[1]
    tiles = beam_ref.shape[2] // LANES
    slot_tiles = col_ref.shape[0]
    rest = slot_tiles - trips * TRIP
    depth = wig_buf.shape[0]
    half = orders * cycles
    by_rows = 2 * half > MXU_ROWS

    def wig_copy(trip, slot):
        lanes = pl.ds(pl.multiple_of(trip * (TRIP * LANES), LANES), TRIP * LANES)
        return pltpu.make_async_copy(wig_hbm.at[:, :, lanes], wig_buf.at[slot], sems.at[slot])

    def tail_copy():
        lanes = pl.ds(trips * TRIP * LANES, rest * LANES)
        return pltpu.make_async_copy(wig_hbm.at[:, :, lanes], tail_buf, tail_sem)

    for trip in range(min(depth - 1, trips)):
        wig_copy(trip, trip).start()
    if rest:
        tail_copy().start()

    low, top = pick_span(col_ref, ell_ref, tiles)
    span = top - low + 1
    row16 = lax.broadcasted_iota(jnp.int32, (16, LANES), 0).astype(jnp.float32).astype(jnp.bfloat16)

    def coeffs(count, first, tile, rows, coeff):
        degree = ell_ref[pl.ds(tile, rows), :]
        sky_re = sky_ref[pl.ds(2 * tile, rows, stride=2), :]
        sky_im = sky_ref[pl.ds(2 * tile + 1, rows, stride=2), :]
        high = (degree >> 7) - first
        index = degree & (LANES - 1)
        here = [high == t for t in range(1, count)]

        def pick(part, order):
            picked = None
            for t in range(count):
                lanes = pl.ds(pl.multiple_of((first + t) * LANES, LANES), LANES)
                entry = jnp.broadcast_to(beam_ref[part, pl.ds(order, 1), lanes], (rows, LANES))
                value = lane_pick(entry, index)
                picked = value if t == 0 else jnp.where(here[t - 1], value, picked)
            return picked

        for order in range(orders):
            real = pick(0, order)
            imag = pick(1, order)
            coeff[order, pl.ds(0, rows), :] = sky_re * real - sky_im * imag
            coeff[orders + order, pl.ds(0, rows), :] = sky_re * imag + sky_im * real

    def values(wig, coeff, part, start, line):
        out = []
        for order in range(orders):
            here = wig[order, :, pl.ds(start, LANES)].astype(jnp.float32)
            row = coeff[part * orders + order, pl.ds(line, 1), :]
            out.append(here * jnp.broadcast_to(row, (cycles, LANES)))
        return jnp.concatenate(out, axis=0)

    def hot(tile):
        line = jnp.broadcast_to(col_ref[pl.ds(tile, 1), :], (16, LANES))
        away = line.astype(jnp.float32).astype(jnp.bfloat16) - row16
        one, zero = jnp.ones_like(away), jnp.zeros_like(away)
        out = [jnp.where(away == jnp.bfloat16(16 * g), one, zero) for g in range(cols // 16)]
        out += [zero] * (MXU // 16 - cols // 16)
        return jnp.concatenate(out, axis=0)

    def body(acc0, acc1):
        accs = (acc0, acc1)
        if by_rows:
            work = lambda i: [(0, i % 2, (0,)), (1, i % 2, (1,))]
        else:
            work = lambda i: [(i % 2, i // 2 % 2, (0, 1))]

        ahead = 1 if by_rows else 2

        def push(i, tile, count=2):
            left = hot(tile)
            right = hot(tile + 1) if count == 2 else jnp.zeros_like(left)
            both = jnp.concatenate([left, right], axis=1)
            for mxu, register, _ in work(i):
                pltpu.matmul_push_rhs(both, register, mxu, transpose=True)

        def multiply(i, wig, coeff, start, line, count=2):
            for mxu, register, parts in work(i):
                blocks = []
                for part in parts:
                    left = values(wig, coeff, part, start, line)
                    if count == 2:
                        right = values(wig, coeff, part, start + LANES, line + 1)
                    else:
                        right = jnp.zeros_like(left)
                    blocks.append(jnp.concatenate([left, right], axis=1))
                block = blocks[0] if len(blocks) == 1 else jnp.concatenate(blocks, axis=0)
                pltpu.matmul_acc_lhs(accs[mxu], block, load_staged_rhs=register)

        pairs = TRIP // 2
        tail_pairs = -(-rest // 2)

        def tail_size(i):
            return min(2, rest - 2 * i)

        def run(count, first):
            coeffs(count, first, 0, SUBLANES, coeff_refs[0])
            for i in range(ahead):
                push(i, 2 * i)

            def trip_body(trip, last):
                slot = lax.rem(trip, depth)
                wig_copy(trip, slot).wait()
                wig = wig_buf.at[slot]
                base = trip * TRIP
                for i in range(pairs):
                    which = 2 * i // SUBLANES
                    if 2 * i % SUBLANES == 0:
                        later = base + (which + 1) * SUBLANES
                        if not last or which + 1 < TRIP // SUBLANES:
                            coeffs(count, first, pl.multiple_of(later, SUBLANES), SUBLANES, coeff_refs[1 - which])
                        else:
                            lines = min(rest, SUBLANES)
                            if lines:
                                coeffs(count, first, trips * TRIP, lines, coeff_refs[0])
                    multiply(i, wig, coeff_refs[which], 2 * i * LANES, 2 * i % SUBLANES)
                    after = i + ahead
                    if not last or after < pairs:
                        push(after, base + 2 * after)
                    elif after - pairs < tail_pairs:
                        push(after, base + 2 * after, tail_size(after - pairs))

            @pl.loop(0, trips - 1)
            def _(trip):
                @pl.when(trip + depth - 1 < trips)
                def _():
                    wig_copy(trip + depth - 1, lax.rem(trip + depth - 1, depth)).start()

                trip_body(trip, False)

            trip_body(trips - 1, True)
            if rest:
                tail_copy().wait()
            for i in range(tail_pairs):
                tile = trips * TRIP + 2 * i
                if 2 * i == SUBLANES:
                    coeffs(count, first, tile, rest - SUBLANES, coeff_refs[1])
                which = 2 * i // SUBLANES
                multiply(pairs + i, tail_buf, coeff_refs[which], 2 * i * LANES, 2 * i % SUBLANES, tail_size(i))
                if ahead + i < tail_pairs:
                    push(pairs + i + ahead, tile + 2 * ahead, tail_size(i + ahead))

        counts = sorted({min(c, tiles) for c in (4, 9)})
        below = 0
        for count in counts:
            first = jnp.minimum(low, tiles - count)

            @pl.when((span > below) & (span <= count) if below else span <= count)
            def _():
                run(count, first)

            below = count
        if below < tiles:

            @pl.when(span > below)
            def _():
                run(tiles, 0)

        if by_rows:
            out_ref[pl.ds(0, half), :] = pltpu.matmul_pop(acc0)[:, :cols]
            out_ref[pl.ds(half, half), :] = pltpu.matmul_pop(acc1)[:, :cols]
        else:
            out_ref[...] = (pltpu.matmul_pop(acc0) + pltpu.matmul_pop(acc1))[:, :cols]

    rows = half if by_rows else 2 * half
    pl.run_scoped(body, pltpu.ACC(0)((rows, MXU), jnp.float32), pltpu.ACC(1)((rows, MXU), jnp.float32))


def order_sums(wigner, sky_alm, beam_blm, slot_col, slot_ell, cols):
    cycles, orders, slots = wigner.shape
    tiles = slots // LANES
    trips = tiles // TRIP
    rest = tiles - trips * TRIP
    depth = 8
    rows = orders * 2 * cycles
    whole = lambda shape: pl.BlockSpec(shape, lambda: (0,) * len(shape))
    sky = sky_alm.reshape(2, tiles, LANES).transpose(1, 0, 2).reshape(2 * tiles, LANES)
    wig = pltpu.with_memory_space_constraint(wigner.transpose(1, 0, 2), pltpu.HBM)
    return pl.pallas_call(
        functools.partial(sums_kernel, orders, cols, trips),
        out_shape=jax.ShapeDtypeStruct((rows, cols), jnp.float32),
        in_specs=[
            pl.BlockSpec(memory_space=pltpu.HBM),
            whole((2 * tiles, LANES)),
            whole((tiles, LANES)),
            whole((tiles, LANES)),
            whole(beam_blm.shape),
        ],
        out_specs=whole((rows, cols)),
        scratch_shapes=[
            pltpu.VMEM((depth, orders, cycles, TRIP * LANES), jnp.bfloat16),
            pltpu.VMEM((orders, cycles, max(rest, 1) * LANES), jnp.bfloat16),
            *[pltpu.VMEM((2 * orders, SUBLANES, LANES), jnp.float32) for _ in range(2)],
            pltpu.SemaphoreType.DMA((depth,)),
            pltpu.SemaphoreType.DMA,
        ],
        compiler_params=pltpu.CompilerParams(vmem_limit_bytes=48 * 1024 * 1024),
        name="order_sums",
    )(wig, sky, slot_col.reshape(tiles, LANES), slot_ell.reshape(tiles, LANES), beam_blm)


def on_device(wigner, sky_alm, beam_blm, slot_col, slot_ell, order_of_column):
    cycle_total = wigner.shape[0]
    order_count = wigner.shape[1]
    blk_count = lax.axis_size("blk")
    col_count = order_of_column.shape[0] // blk_count
    col_sums = order_sums(wigner, sky_alm, beam_blm, slot_col, slot_ell, col_count)
    by_cycle = col_sums.reshape(2, order_count, cycle_total, col_count).transpose(2, 0, 1, 3)
    ell_count = lax.axis_size("ell")
    partials = by_cycle.reshape((ell_count, cycle_total // ell_count) + by_cycle.shape[1:])
    summed = lax.all_to_all(partials, "ell", split_axis=0, concat_axis=0, tiled=True).sum(axis=0)
    owned = jnp.einsum(
        "trkc,rksp->tspc",
        summed,
        psi_table(order_count, NPSI),
        precision=lax.Precision.HIGHEST,
    )
    return to_phi(
        lax.all_to_all(owned, "blk", split_axis=2, concat_axis=3, tiled=True), order_of_column
    )


def solution(mesh):
    return jax.shard_map(
        on_device,
        mesh=mesh,
        in_specs=(
            P(None, None, ("ell", "blk")),
            P(None, ("ell", "blk")),
            P(),
            P(("ell", "blk")),
            P(("ell", "blk")),
            P(),
        ),
        out_specs=P("ell", "blk", None),
        check_vma=False,
    )
```

time: 84.6 us -> 63.6 us (0.75)
  Pallas kernels: 47.7 us -> 27.4 us
    pallas_call x1, Pallas kernels: 47.7 us -> 27.4 us  [order_sums(): pl.pallas_call(functools.partial(sums_kernel, orders, cols, trips), out_s...]
    broadcast_in_dim x2 -> x0, local copies, waits for them, and re-layouts: 2.27 us -> none  [the longest x1 1.13 us: order_sums(): slot_col[None, :]]
    unnamed x4 -> x7, local copies, waits for them, and re-layouts: 1.04 us -> 3.03 us
    reshape x1 -> x3, local copies, waits for them, and re-layouts: 0.14 us -> 1.97 us  [the longest x2 1.82 us: order_sums(): sky_alm.reshape(2, tiles, LANES).transpose(1, 0, 2)]
    all_to_all x1, starting transfers between devices: 4.89 us -> 3.45 us  [on_device(): lax.all_to_all(partials, 'ell', split_axis=0, concat_axis=0, tiled=True)]
    slice x1 -> x0, local copies, waits for them, and re-layouts: 1.34 us -> none  [beam_table(): rows = [beam[0, :whole], beam[1, :whole]]]
  transfers between devices with their start and end apart: 2 -> 2, of which waited for: 2 -> 2; matrix products, arithmetic and copies ran while one was open for 3% -> 4% of each run, Pallas kernels for 0% -> 0%
where the time goes in v1:
time: 63.6 us; the launch traced here: 63.2 us
  Pallas kernels  27.4 us (43%)
  waiting for transfers between devices  10.3 us (16%)
  starting transfers between devices  9.28 us (15%)
  local copies, waits for them, and re-layouts  7.98 us (13%)
  matrix products  5.45 us (9%)
  other arithmetic  2.61 us (4%)
    pallas_call x1, Pallas kernels, order_sums(): pl.pallas_call(functools.partial(sums_kernel, orders, cols, trips), out_s...  27.4 us
    all_to_all x1, waiting for transfers between devices, on_device(): lax.all_to_all(partials, 'ell', split_axis=0, concat_axis=0, tiled=True)  6.07 us
    all_to_all x1, starting transfers between devices, on_device(): lax.all_to_all(owned, 'blk', split_axis=2, concat_axis=3, tiled=True)  5.83 us
    all_to_all x1, waiting for transfers between devices, on_device(): lax.all_to_all(owned, 'blk', split_axis=2, concat_axis=3, tiled=True)  4.25 us
    all_to_all x1, starting transfers between devices, on_device(): lax.all_to_all(partials, 'ell', split_axis=0, concat_axis=0, tiled=True)  3.45 us
    unnamed x7, local copies, waits for them, and re-layouts  3.03 us
    dot_general x1, matrix products, to_phi(): jnp.einsum('tpcj,cv->tpvj', weighted_im, select, precision=highest)  2.14 us
    dot_general x1, matrix products, to_phi(): jnp.einsum('tpcj,cv->tpvj', weighted_re, select, precision=highest)  2.14 us
  transfers between devices with their start and end apart: 2, of which 2 were waited for; matrix products, arithmetic and copies ran while one was open for 4% of the time, Pallas kernels for 0%

profile of v1, /device:TPU:0, one launch (start us, length us, event | category | flops | bytes accessed | tf_op | source)
XLA Modules:
  0.0 63.2 jit_solution(8442989538863040615)
XLA Ops:
  0.0 1.5 %reshape.182 = f32[2,513,128]{2,1,0:T(8,128)S(1)} reshape(f32[2,65664]{1,0:T(2,128)} %param.7) | data formatting | bytes 1050624 | tf_op jit(solution)/shard_map/reshape | solution.py:276
  1.5 0.3 copy.26
  1.7 0.4 reshape.183.sky_ref
  2.1 1.1 %copy.27.beam_ref = f32[2,17,2048]{2,1,0:T(8,128)S(1)} copy(f32[2,17,2048]{2,0,1:T(2,128)} %param.8) | data formatting | bytes 557056 | tf_op args[2]
  3.3 0.9 %copy-done = s32[65664]{0:T(1024)S(1)} copy-done((s32[65664]{0:T(1024)S(1)}, s32[65664]{0:T(1024)}, u32[]{:S(2)}) %copy-start) | copy-done | bytes 262680
  4.2 0.9 %copy-done.1 = s32[65664]{0:T(1024)S(1)} copy-done((s32[65664]{0:T(1024)S(1)}, s32[65664]{0:T(1024)}, u32[]{:S(2)}) %copy-start.1) | copy-done | bytes 262680
  5.2 27.4 %order_sums.1 = f32[272,256]{1,0:T(8,128)S(1)} custom-call(bf16[17,8,65664]{2,1,0:T(8,128)(2,1)} %bitcast.66, f32[1026,128]{1,0:T(8,128)S(1)} %reshape.183.sky_ref, s32[513,128]{1,0:T(8,128)S(1)} %bitcast.64, s32[513,128]{1,0:T(8,128)S(1)} %bitcast.65, f32[2,17,2048]{2,1,0:T(8,128)S(1)} %copy.27.beam_ref), custom_call_target="tpu_custom_call" | custom-call | tf_op jit(solution)/shard_map/order_sums/pallas_call | solution.py:278
  32.5 0.1 copy.28
  32.7 0.9 %copy.29 = f32[4,2,2,17,256]{4,1,3,2,0:T(2,128)} copy(f32[4,2,2,17,256]{4,2,3,1,0:T(2,128)S(1)} %bitcast.68) | data formatting | bytes 557056 | tf_op jit(solution)/shard_map/reshape | solution.py:309
  33.6 3.4 %all-to-all-start = ((f32[4,2,2,17,256]{4,1,3,2,0:T(2,128)}), f32[4,2,2,17,256]{4,1,3,2,0:T(2,128)S(1)}, u32[]{:S(2)}, u32[]{:S(2)}) async-start(f32[4,2,2,17,256]{4,1,3,2,0:T(2,128)} %copy.29), calls=%async_computation | async-start | bytes 557056 | tf_op jit(solution)/shard_map/all_to_all | solution.py:310
  37.2 6.1 %all-to-all-done = f32[4,2,2,17,256]{4,1,3,2,0:T(2,128)S(1)} async-done(((f32[4,2,2,17,256]{4,1,3,2,0:T(2,128)}), f32[4,2,2,17,256]{4,1,3,2,0:T(2,128)S(1)}, u32[]{:S(2)}, u32[]{:S(2)}) %all-to-all-start) | async-done | bytes 278560 | tf_op jit(solution)/shard_map/all_to_all | solution.py:310
  43.3 0.1 reduce_sum.9
  43.4 0.3 convolution_bitcast_fusion
  43.7 0.8 %copy.32 = f32[2,2,32,256]{3,0,1,2:T(2,128)} copy(f32[2,2,32,256]{3,2,0,1:T(8,128)S(1)} %convolution_bitcast_fusion) | data formatting | bytes 262144 | tf_op jit(solution)/shard_map/trkc,rksp->tspc/transpose | solution.py:311
  44.5 5.8 %all-to-all-start.1 = ((f32[2,2,32,256]{3,0,1,2:T(2,128)}), f32[2,2,32,256]{3,0,1,2:T(2,128)S(1)}, u32[]{:S(2)}, u32[]{:S(2)}) async-start(f32[2,2,32,256]{3,0,1,2:T(2,128)} %copy.32), calls=%async_computation.1 | async-start | bytes 262144 | tf_op jit(solution)/shard_map/all_to_all | solution.py:318
  50.3 2.0 %fusion.36 = (f32[2048,64]{0,1:T(8,128)S(1)}, f32[2048,64]{0,1:T(8,128)S(1)}) fusion(s32[2048]{0:T(1024)S(1)} %get-tuple-element.10), kind=kLoop, calls=%fused_computation.40 | loop fusion | flops 1835008 | bytes 1056768 | tf_op jit(solution)/shard_map/cos | solution.py:48
  52.4 0.1 fusion.63
  52.6 0.2 fusion.62
  52.8 4.3 %all-to-all-done.1 = f32[2,2,32,256]{3,0,1,2:T(2,128)S(1)} async-done(((f32[2,2,32,256]{3,0,1,2:T(2,128)}), f32[2,2,32,256]{3,0,1,2:T(2,128)S(1)}, u32[]{:S(2)}, u32[]{:S(2)}) %all-to-all-start.1) | async-done | bytes 131104 | tf_op jit(solution)/shard_map/all_to_all | solution.py:318
  57.2 2.1 %fusion.4 = f32[64,2,4,64]{3,0,2,1:T(8,128)S(1)} fusion(f32[2048,64]{0,1:T(8,128)S(1)} %get-tuple-element.12, f32[2,4,2048]{2,1,0:T(4,128)S(1)} %get-tuple-element.6, f32[2048,64]{0,1:T(8,128)S(1)} %get-tuple-element.11, f32[2,4,2048]{2,1,0:T(4,128)S(1)} %get-tuple-element.5, s32[2048]{0:T(1024)S(1)} %get-tuple-element.9), kind=kOutput, calls=%fused_computation.4 | convolution fusion | flops 405929984 | bytes 1318912 | tf_op jit(solution)/shard_map/tpcj,cv->tpvj/dot_general | solution.py:55
  59.4 2.1 %fusion = f32[64,2,4,64]{3,0,2,1:T(8,128)S(1)} fusion(f32[2048,64]{0,1:T(8,128)S(1)} %get-tuple-element.12, f32[2,4,2048]{2,1,0:T(4,128)S(1)} %get-tuple-element.6, f32[2048,64]{0,1:T(8,128)S(1)} %get-tuple-element.11, f32[2,4,2048]{2,1,0:T(4,128)S(1)} %get-tuple-element.5, s32[2048]{0:T(1024)S(1)} %get-tuple-element.9), kind=kOutput, calls=%fused_computation | convolution fusion | flops 405929984 | bytes 1318912 | tf_op jit(solution)/shard_map/tpcj,cv->tpvj/dot_general | solution.py:56
  61.5 0.4 fusion.27
  62.0 0.4 fusion.16
  62.4 0.8 %reshape.188 = f32[2,4,4096]{2,1,0:T(4,128)} reshape(f32[2,4,64,64]{3,2,1,0:T(8,128)S(1)} %fusion.16) | data formatting | bytes 262144 | tf_op jit(solution)/shard_map/reshape | solution.py:64
  (13 shorter events, 0.5 us)
Async XLA Ops:
  3.2 1.0 %copy-start = (s32[65664]{0:T(1024)S(1)}, s32[65664]{0:T(1024)}, u32[]{:S(2)}) copy-start(s32[65664]{0:T(1024)} %param.9) | copy-start | bytes 787972
  4.2 1.0 %copy-start.1 = (s32[65664]{0:T(1024)S(1)}, s32[65664]{0:T(1024)}, u32[]{:S(2)}) copy-start(s32[65664]{0:T(1024)} %param.10) | copy-start | bytes 787972
  5.2 32.0 %copy-start.2 = (s32[2048]{0:T(1024)S(1)}, s32[2048]{0:T(1024)}, u32[]{:S(2)}) copy-start(s32[2048]{0:T(1024)} %param.11) | copy-start | bytes 24580
  33.6 9.7 %all-to-all-start = ((f32[4,2,2,17,256]{4,1,3,2,0:T(2,128)}), f32[4,2,2,17,256]{4,1,3,2,0:T(2,128)S(1)}, u32[]{:S(2)}, u32[]{:S(2)}) async-start(f32[4,2,2,17,256]{4,1,3,2,0:T(2,128)} %copy.29), calls=%async_computation | async-start | bytes 557056 | tf_op jit(solution)/shard_map/all_to_all | solution.py:310
  44.5 12.6 %all-to-all-start.1 = ((f32[2,2,32,256]{3,0,1,2:T(2,128)}), f32[2,2,32,256]{3,0,1,2:T(2,128)S(1)}, u32[]{:S(2)}, u32[]{:S(2)}) async-start(f32[2,2,32,256]{3,0,1,2:T(2,128)} %copy.32), calls=%async_computation.1 | async-start | bytes 262144 | tf_op jit(solution)/shard_map/all_to_all | solution.py:318

commit v2 on v1

v2 whole, which is shorter than its diff:
```python
import functools
import math

import jax
import jax.numpy as jnp
import numpy as np
from jax import lax
from jax.experimental import pallas as pl
from jax.experimental.pallas import tpu as pltpu
from jax.sharding import PartitionSpec as P

NPSI = 32
LANES = 128
SUBLANES = 8
MXU = 256
MXU_ROWS = 1024
TRIP = 16
MESH = pl.DeviceIdType.MESH


def round_up(value, step):
    return -(-value // step) * step


def lane_pick(table, index):
    return lax.gather(
        table,
        index[..., None],
        lax.GatherDimensionNumbers(
            offset_dims=(),
            collapsed_slice_dims=(1,),
            start_index_map=(1,),
            operand_batching_dims=(0,),
            start_indices_batching_dims=(0,),
        ),
        slice_sizes=(1, 1),
        mode=lax.GatherScatterMode.PROMISE_IN_BOUNDS,
    )


REAL_STEP = 1 << 19
IMAG_SHIFT = 13
POWER_BITS = 6
LEAST_POWER = 62
FULL = 4094.0


def largest(blocks):
    most = functools.reduce(jnp.maximum, [jnp.abs(block) for block in blocks])
    return jnp.max(most, axis=(0, 1), keepdims=True)


def pack_beam(real_ref, imag_ref, table_ref):
    orders, degrees = table_ref.shape
    most = jnp.maximum(largest([real_ref[...], imag_ref[...]]), 1e-30)
    unit = jnp.broadcast_to(1.0 / most, (orders, LANES))
    for tile in range(degrees // LANES):
        lanes = pl.ds(tile * LANES, LANES)
        real, imag = real_ref[:, lanes] * unit, imag_ref[:, lanes] * unit
        size = jnp.maximum(jnp.abs(real), jnp.abs(imag))
        power = jnp.floor(jnp.log2(size)) + 1.0
        power = jnp.minimum(jnp.maximum(power, -float(LEAST_POWER)), 1.0)
        grow = jnp.exp2(-power) * FULL
        code = (power + float(LEAST_POWER)).astype(jnp.int32)
        below = code.astype(jnp.float32) * (1.0 / 64.0)
        imag_code = jnp.floor(imag * grow - below + 0.5).astype(jnp.int32)
        low = ((imag_code & 0x1FFF) << POWER_BITS) + code
        below = low.astype(jnp.float32) * (1.0 / REAL_STEP)
        real_code = jnp.floor(real * grow - below + 0.5).astype(jnp.int32)
        table_ref[:, lanes] = (real_code << 19) + low
    return most


def pick_span(col_ref, ell_ref, tiles):
    live = col_ref[...] >= 0
    degree = ell_ref[...]
    last = tiles * LANES - 1
    top = jnp.max(jnp.where(live, degree, 0).astype(jnp.float32)).astype(jnp.int32)
    low = jnp.min(jnp.where(live, degree, last).astype(jnp.float32)).astype(jnp.int32)
    return low // LANES, top // LANES


def sums_kernel(orders, cols, trips, wig_hbm, sky_hbm, col_hbm, ell_hbm, beam_hbm, out_ref, *scratch):
    wig_buf, tail_buf, sky_ref, col_ref, ell_ref, real_ref, imag_ref, table_ref = scratch[0:8]
    coeff_refs, sems, once = scratch[8:10], scratch[10], scratch[11]
    cycles = wig_hbm.shape[1]
    tiles = table_ref.shape[1] // LANES
    slot_tiles = col_ref.shape[0]
    rest = slot_tiles - trips * TRIP
    depth = wig_buf.shape[0]
    half = orders * cycles
    by_rows = 2 * half > MXU_ROWS

    def wig_copy(trip, slot):
        lanes = pl.ds(pl.multiple_of(trip * (TRIP * LANES), LANES), TRIP * LANES)
        return pltpu.make_async_copy(wig_hbm.at[:, :, lanes], wig_buf.at[slot], sems.at[slot])

    rest_lanes = pl.ds(trips * TRIP * LANES, rest * LANES)
    ell_copy = pltpu.make_async_copy(ell_hbm, ell_ref, once.at[0])
    col_copy = pltpu.make_async_copy(col_hbm, col_ref, once.at[1])
    real_copy = pltpu.make_async_copy(beam_hbm.at[:, 0, :], real_ref, once.at[2])
    imag_copy = pltpu.make_async_copy(beam_hbm.at[:, 1, :], imag_ref, once.at[3])
    sky_copy = pltpu.make_async_copy(sky_hbm, sky_ref, once.at[4])
    for copy in (real_copy, imag_copy, col_copy, ell_copy, sky_copy):
        copy.start()
    for trip in range(min(depth - 1, trips)):
        wig_copy(trip, trip).start()
    if rest:
        tail_copy = pltpu.make_async_copy(wig_hbm.at[:, :, rest_lanes], tail_buf, once.at[5])
        tail_copy.start()

    real_copy.wait()
    imag_copy.wait()
    most = pack_beam(real_ref, imag_ref, table_ref)
    unit = jnp.broadcast_to(most * (1.0 / (REAL_STEP * FULL)), (SUBLANES, LANES))
    col_copy.wait()
    ell_copy.wait()
    low, top = pick_span(col_ref, ell_ref, tiles)
    span = top - low + 1
    sky_copy.wait()
    row16 = lax.broadcasted_iota(jnp.int32, (16, LANES), 0).astype(jnp.float32).astype(jnp.bfloat16)

    def coeffs(count, first, tile, rows, coeff):
        degree = ell_ref[pl.ds(tile, rows), :]
        lanes = pl.ds(pl.multiple_of(tile * LANES, LANES), rows * LANES)
        sky_re = sky_ref[pl.ds(0, 1), lanes].reshape(rows, LANES) * unit[:rows]
        sky_im = sky_ref[pl.ds(1, 1), lanes].reshape(rows, LANES) * unit[:rows]
        high = (degree >> 7) - first
        index = degree & (LANES - 1)
        here = [high == t for t in range(1, count)]
        for order in range(orders):
            word = None
            for t in range(count):
                lanes = pl.ds(pl.multiple_of((first + t) * LANES, LANES), LANES)
                entry = jnp.broadcast_to(table_ref[pl.ds(order, 1), lanes], (rows, LANES))
                value = lane_pick(entry, index)
                word = value if t == 0 else jnp.where(here[t - 1], value, word)
            real = word.astype(jnp.float32)
            imag = (word << IMAG_SHIFT).astype(jnp.float32)
            power = jnp.exp2((word & (2**POWER_BITS - 1)).astype(jnp.float32) - float(LEAST_POWER))
            real, imag = real * power, imag * power
            coeff[order, pl.ds(0, rows), :] = sky_re * real - sky_im * imag
            coeff[orders + order, pl.ds(0, rows), :] = sky_re * imag + sky_im * real

    def values(wig, coeff, part, start, line):
        out = []
        for order in range(orders):
            here = wig[order, :, pl.ds(start, LANES)].astype(jnp.float32)
            row = coeff[part * orders + order, pl.ds(line, 1), :]
            out.append(here * jnp.broadcast_to(row, (cycles, LANES)))
        return jnp.concatenate(out, axis=0)

    def hot(tile):
        line = jnp.broadcast_to(col_ref[pl.ds(tile, 1), :], (16, LANES))
        away = line.astype(jnp.float32).astype(jnp.bfloat16) - row16
        one, zero = jnp.ones_like(away), jnp.zeros_like(away)
        out = [jnp.where(away == jnp.bfloat16(16 * g), one, zero) for g in range(cols // 16)]
        out += [zero] * (MXU // 16 - cols // 16)
        return jnp.concatenate(out, axis=0)

    def body(acc0, acc1):
        accs = (acc0, acc1)
        if by_rows:
            work = lambda i: [(0, i % 2, (0,)), (1, i % 2, (1,))]
        else:
            work = lambda i: [(i % 2, i // 2 % 2, (0, 1))]

        ahead = 1 if by_rows else 2

        def push(i, tile, count=2):
            left = hot(tile)
            right = hot(tile + 1) if count == 2 else jnp.zeros_like(left)
            both = jnp.concatenate([left, right], axis=1)
            for mxu, register, _ in work(i):
                pltpu.matmul_push_rhs(both, register, mxu, transpose=True)

        def multiply(i, wig, coeff, start, line, count=2):
            for mxu, register, parts in work(i):
                blocks = []
                for part in parts:
                    left = values(wig, coeff, part, start, line)
                    if count == 2:
                        right = values(wig, coeff, part, start + LANES, line + 1)
                    else:
                        right = jnp.zeros_like(left)
                    blocks.append(jnp.concatenate([left, right], axis=1))
                block = blocks[0] if len(blocks) == 1 else jnp.concatenate(blocks, axis=0)
                pltpu.matmul_acc_lhs(accs[mxu], block, load_staged_rhs=register)

        pairs = TRIP // 2
        tail_pairs = -(-rest // 2)

        def tail_size(i):
            return min(2, rest - 2 * i)

        def run(count, first):
            coeffs(count, first, 0, SUBLANES, coeff_refs[0])
            for i in range(ahead):
                push(i, 2 * i)

            def trip_body(trip, last):
                slot = lax.rem(trip, depth)
                wig_copy(trip, slot).wait()
                wig = wig_buf.at[slot]
                base = trip * TRIP
                for i in range(pairs):
                    which = 2 * i // SUBLANES
                    if 2 * i % SUBLANES == 0:
                        later = base + (which + 1) * SUBLANES
                        if not last or which + 1 < TRIP // SUBLANES:
                            coeffs(count, first, pl.multiple_of(later, SUBLANES), SUBLANES, coeff_refs[1 - which])
                        else:
                            lines = min(rest, SUBLANES)
                            if lines:
                                coeffs(count, first, trips * TRIP, lines, coeff_refs[0])
                    multiply(i, wig, coeff_refs[which], 2 * i * LANES, 2 * i % SUBLANES)
                    after = i + ahead
                    if not last or after < pairs:
                        push(after, base + 2 * after)
                    elif after - pairs < tail_pairs:
                        push(after, base + 2 * after, tail_size(after - pairs))

            @pl.loop(0, trips - 1)
            def _(trip):
                @pl.when(trip + depth - 1 < trips)
                def _():
                    wig_copy(trip + depth - 1, lax.rem(trip + depth - 1, depth)).start()

                trip_body(trip, False)

            trip_body(trips - 1, True)
            if rest:
                tail_copy.wait()
            for i in range(tail_pairs):
                tile = trips * TRIP + 2 * i
                if 2 * i == SUBLANES:
                    coeffs(count, first, tile, rest - SUBLANES, coeff_refs[1])
                which = 2 * i // SUBLANES
                multiply(pairs + i, tail_buf, coeff_refs[which], 2 * i * LANES, 2 * i % SUBLANES, tail_size(i))
                if ahead + i < tail_pairs:
                    push(pairs + i + ahead, tile + 2 * ahead, tail_size(i + ahead))

        counts = sorted({min(c, tiles) for c in (4, 9)})
        below = 0
        for count in counts:
            first = jnp.minimum(low, tiles - count)

            @pl.when((span > below) & (span <= count) if below else span <= count)
            def _():
                run(count, first)

            below = count
        if below < tiles:

            @pl.when(span > below)
            def _():
                run(tiles, 0)

        groups = round_up(2 * orders, SUBLANES)
        width = out_ref.shape[2]
        sums = [pltpu.matmul_pop(acc0), pltpu.matmul_pop(acc1)]
        if not by_rows:
            sums = [sums[0] + sums[1]]
        sums = jnp.concatenate(sums, axis=0)
        for piece in range(cols // width):
            lanes = slice(piece * width, (piece + 1) * width)
            for cycle in range(cycles):
                if groups > 2 * orders:
                    pad = pl.ds(cycle * groups + 2 * orders, groups - 2 * orders)
                    out_ref[piece, pad, :] = jnp.zeros((groups - 2 * orders, width), jnp.float32)
            for row in range(2 * orders):
                for cycle in range(0, cycles, SUBLANES):
                    here = pl.ds(cycle * groups + row, SUBLANES, stride=groups)
                    start = row * cycles + cycle
                    out_ref[piece, here, :] = sums[start : start + SUBLANES, lanes]

    rows = half if by_rows else 2 * half
    pl.run_scoped(body, pltpu.ACC(0)((rows, MXU), jnp.float32), pltpu.ACC(1)((rows, MXU), jnp.float32))


def order_sums(wigner, sky_alm, beam_blm, slot_col, slot_ell, cols):
    cycles, orders, slots = wigner.shape
    degrees = beam_blm.shape[2]
    tiles = slots // LANES
    trips = tiles // TRIP
    rest = tiles - trips * TRIP
    depth = 8
    width = min(cols, LANES)
    shape = (cols // width, cycles * round_up(2 * orders, SUBLANES), width)
    in_hbm = lambda x: pltpu.with_memory_space_constraint(x, pltpu.HBM)
    return pl.pallas_call(
        functools.partial(sums_kernel, orders, cols, trips),
        out_shape=jax.ShapeDtypeStruct(shape, jnp.float32),
        in_specs=[pl.BlockSpec(memory_space=pltpu.HBM)] * 5,
        out_specs=pl.BlockSpec(memory_space=pltpu.VMEM),
        scratch_shapes=[
            pltpu.VMEM((depth, orders, cycles, TRIP * LANES), jnp.bfloat16),
            pltpu.VMEM((orders, cycles, max(rest, 1) * LANES), jnp.bfloat16),
            pltpu.VMEM((2, slots), jnp.float32),
            pltpu.VMEM((tiles, LANES), jnp.int32),
            pltpu.VMEM((tiles, LANES), jnp.int32),
            pltpu.VMEM((orders, degrees), jnp.float32),
            pltpu.VMEM((orders, degrees), jnp.float32),
            pltpu.VMEM((orders, degrees), jnp.int32),
            *[pltpu.VMEM((2 * orders, SUBLANES, LANES), jnp.float32) for _ in range(2)],
            pltpu.SemaphoreType.DMA((depth,)),
            pltpu.SemaphoreType.DMA((6,)),
        ],
        compiler_params=pltpu.CompilerParams(vmem_limit_bytes=32 * 1024 * 1024),
        name="order_sums",
    )(
        in_hbm(wigner.transpose(1, 0, 2)),
        in_hbm(sky_alm),
        in_hbm(slot_col.reshape(tiles, LANES)),
        in_hbm(slot_ell.reshape(tiles, LANES)),
        in_hbm(beam_blm.transpose(1, 0, 2)),
    )


def split(value):
    high = value.astype(jnp.bfloat16)
    return high, (value - high.astype(jnp.float32)).astype(jnp.bfloat16)


def split_table(table):
    high, low = split(jnp.asarray(table, jnp.float32))
    return jnp.stack([high, low])


def product(left, right):
    dot = functools.partial(jnp.dot, preferred_element_type=jnp.float32)
    return dot(left[0], right[0]) + dot(left[0], right[1]) + dot(left[1], right[0])


def psi_rows(orders, blks, turns, samples):
    groups, lines = round_up(2 * orders, SUBLANES), round_up(turns * samples, SUBLANES)
    table = np.zeros((blks, 2, lines, turns, groups))
    sample = np.arange(blks * samples).reshape(blks, samples)
    angle = 2.0 * np.pi * (sample[..., None] * np.arange(orders) % (blks * samples)) / (blks * samples)
    for turn in range(turns):
        rows = slice(turn * samples, (turn + 1) * samples)
        table[:, 0, rows, turn, :orders] = np.cos(angle)
        table[:, 0, rows, turn, orders : 2 * orders] = -np.sin(angle)
        table[:, 1, rows, turn, :orders] = np.sin(angle)
        table[:, 1, rows, turn, orders : 2 * orders] = np.cos(angle)
    return table.reshape(blks * 2 * lines, turns * groups)


def exchange_kernel(turns, lines, sums_ref, table_ref, order_ref, all_ref, from_ref, *scratch):
    recv, out, sum_send, sum_recv, all_send, all_recv = scratch
    ells, blks = lax.axis_size("ell"), lax.axis_size("blk")
    ell, blk = lax.axis_index("ell"), lax.axis_index("blk")
    pieces, _, width = sums_ref.shape
    rows = recv.shape[2]
    block = 2 * lines

    barrier = pltpu.get_barrier_semaphore()
    for step in range(1, ells):
        pl.semaphore_signal(barrier, inc=1, device_id={"ell": lax.rem(ell + step, ells)}, device_id_type=MESH)
    for step in range(1, blks):
        pl.semaphore_signal(barrier, inc=1, device_id={"blk": lax.rem(blk + step, blks)}, device_id_type=MESH)
    pl.semaphore_wait(barrier, ells + blks - 2)

    def sum_copy(piece, step):
        target = lax.rem(ell + step, ells)
        return pltpu.make_async_remote_copy(
            src_ref=sums_ref.at[piece, pl.ds(pl.multiple_of(target * rows, SUBLANES), rows), :],
            dst_ref=recv.at[step - 1, piece],
            send_sem=sum_send.at[piece, step - 1],
            recv_sem=sum_recv.at[piece, step - 1],
            device_id={"ell": target},
            device_id_type=MESH,
        )

    def all_copy(piece, step):
        target = lax.rem(blk + step, blks)
        return pltpu.make_async_remote_copy(
            src_ref=out.at[piece, pl.ds(pl.multiple_of(target * block, SUBLANES), block), :],
            dst_ref=all_ref.at[blk, piece],
            send_sem=all_send.at[piece, step - 1],
            recv_sem=all_recv.at[piece, step - 1],
            device_id={"blk": target},
            device_id_type=MESH,
        )

    for piece in range(pieces):
        for step in range(1, ells):
            sum_copy(piece, step).start()

    order = order_ref[...]
    total = order.shape[1]
    first = from_ref.shape[0] * 2
    span = total // first
    place = (order % first) // 2
    lane = (order % 2) * span + order // first
    column = lax.broadcasted_iota(jnp.int32, (from_ref.shape[0], total), 1)
    here = lax.broadcasted_iota(jnp.int32, (from_ref.shape[0], total), 0) == place
    pick = lambda x: jnp.where(here, x, 0).astype(jnp.float32).astype(jnp.bfloat16)
    left = jnp.concatenate([pick(column // 16), pick(column % 16)], axis=0)
    right = lax.broadcasted_iota(jnp.int32, (LANES, total), 0) == lane
    right = right.astype(jnp.float32).astype(jnp.bfloat16)
    found = lax.dot_general(left, right, (((1,), (1,)), ((), ())), preferred_element_type=jnp.float32)
    half = from_ref.shape[0]
    from_ref[...] = (found[:half] * 16.0 + found[half:]).astype(jnp.int32)

    table = (table_ref[0], table_ref[1])
    for piece in range(pieces):
        total = sums_ref[piece, pl.ds(pl.multiple_of(ell * rows, SUBLANES), rows), :]
        for step in range(1, ells):
            sum_copy(piece, step).wait_recv()
            total = total + recv[step - 1, piece]
        out[piece] = product(table, split(total))
        for step in range(1, blks):
            all_copy(piece, step).start()
        all_ref[blk, piece] = out[piece, pl.ds(pl.multiple_of(blk * block, SUBLANES), block), :]

    for piece in range(pieces):
        for step in range(1, blks):
            all_copy(piece, step).wait_recv()
    for piece in range(pieces):
        for step in range(1, ells):
            sum_copy(piece, step).wait_send()
        for step in range(1, blks):
            all_copy(piece, step).wait_send()


def exchange(sums, order_of_column, orders, cycles):
    ells, blks = lax.axis_size("ell"), lax.axis_size("blk")
    pieces, _, width = sums.shape
    turns, samples = cycles // ells, NPSI // blks
    lines = round_up(turns * samples, SUBLANES)
    rows = turns * round_up(2 * orders, SUBLANES)
    total = order_of_column.shape[0]
    table = split_table(psi_rows(orders, blks, turns, samples))
    in_vmem = pl.BlockSpec(memory_space=pltpu.VMEM)
    return pl.pallas_call(
        functools.partial(exchange_kernel, turns, lines),
        out_shape=(
            jax.ShapeDtypeStruct((blks, pieces, 2 * lines, width), jnp.float32),
            jax.ShapeDtypeStruct((total // LANES, LANES), jnp.int32),
        ),
        in_specs=[in_vmem] * 3,
        out_specs=(in_vmem, in_vmem),
        scratch_shapes=[
            pltpu.VMEM((ells - 1, pieces, rows, width), jnp.float32),
            pltpu.VMEM((pieces, blks * 2 * lines, width), jnp.float32),
            pltpu.SemaphoreType.DMA((pieces, ells - 1)),
            pltpu.SemaphoreType.DMA((pieces, ells - 1)),
            pltpu.SemaphoreType.DMA((pieces, blks - 1)),
            pltpu.SemaphoreType.DMA((pieces, blks - 1)),
        ],
        compiler_params=pltpu.CompilerParams(
            collective_id=0, has_side_effects=True, vmem_limit_bytes=32 * 1024 * 1024
        ),
        name="exchange",
    )(sums, table, order_of_column[None, :])


def turned(value, turn, period):
    real, imag = value
    turn = turn % period
    if turn == 0:
        return real, imag
    if 4 * turn == period:
        return -imag, real
    cos, sin = math.cos(2.0 * math.pi * turn / period), math.sin(2.0 * math.pi * turn / period)
    return real * cos - imag * sin, real * sin + imag * cos


def transform(values):
    size = len(values)
    if size == 1:
        return values
    even, odd = transform(values[0::2]), transform(values[1::2])
    odd = [turned(value, j, size) for j, value in enumerate(odd)]
    low = [(e[0] + o[0], e[1] + o[1]) for e, o in zip(even, odd)]
    high = [(e[0] - o[0], e[1] - o[1]) for e, o in zip(even, odd)]
    return low + high


def phi_kernel(lines, all_ref, from_ref, table_ref, twist_ref, out_ref):
    turns, samples, _ = out_ref.shape
    blks, pieces, _, width = all_ref.shape
    places = from_ref.shape[0]
    per = LANES // width
    real, imag = [], []
    blocks = [(b, piece) for b in range(blks) for piece in range(pieces)]
    for tile in range(len(blocks) // per):
        for rows, into in ((pl.ds(0, lines), real), (pl.ds(lines, lines), imag)):
            part = [all_ref[b, piece, rows, :] for b, piece in blocks[tile * per : (tile + 1) * per]]
            into.append(part[0] if per == 1 else jnp.concatenate(part, axis=1))
    rows = []
    for place in range(places):
        source = jnp.broadcast_to(from_ref[pl.ds(place, 1), :], (lines, LANES))
        high, index = source >> 7, source & (LANES - 1)
        both = []
        for tiles in (real, imag):
            picked = lane_pick(tiles[0], index)
            for t in range(1, len(tiles)):
                picked = jnp.where(high == t, lane_pick(tiles[t], index), picked)
            both.append(picked)
        rows.append(jnp.concatenate(both, axis=1))
    first = product(split(jnp.concatenate(rows, axis=0)), (table_ref[0], table_ref[1]))
    values = []
    for place in range(places):
        here = first[place * lines : (place + 1) * lines]
        for side in range(2):
            re = here[:, 2 * side * LANES : (2 * side + 1) * LANES]
            im = here[:, (2 * side + 1) * LANES : (2 * side + 2) * LANES]
            cos = jnp.broadcast_to(twist_ref[0, pl.ds(2 * place + side, 1), :], (lines, LANES))
            sin = jnp.broadcast_to(twist_ref[1, pl.ds(2 * place + side, 1), :], (lines, LANES))
            values.append((re * cos - im * sin, re * sin + im * cos))
    for j, (value, _) in enumerate(transform(values)):
        for turn in range(turns):
            out_ref[turn, :, j * LANES : (j + 1) * LANES] = value[turn * samples : (turn + 1) * samples]


def phi_tables(degrees):
    outer = 2 * degrees // LANES
    span = degrees // outer
    angle = 2.0 * np.pi * np.outer(np.arange(span), np.arange(LANES)) / LANES
    table = np.zeros((2, 2, span, 2, 2, LANES))
    for side in range(2):
        table[0, side, :, side, 0] = np.cos(angle)
        table[0, side, :, side, 1] = np.sin(angle)
        table[1, side, :, side, 0] = -np.sin(angle)
        table[1, side, :, side, 1] = np.cos(angle)
    angle = 2.0 * np.pi * np.outer(np.arange(outer), np.arange(LANES)) / (2 * degrees)
    return table.reshape(4 * span, 4 * LANES), np.stack([np.cos(angle), np.sin(angle)])


def to_phi(gathered, origin, turns, samples, degrees):
    table, twist = phi_tables(degrees)
    in_vmem = pl.BlockSpec(memory_space=pltpu.VMEM)
    return pl.pallas_call(
        functools.partial(phi_kernel, gathered.shape[2] // 2),
        out_shape=jax.ShapeDtypeStruct((turns, samples, 2 * degrees), jnp.float32),
        in_specs=[in_vmem] * 4,
        out_specs=in_vmem,
        compiler_params=pltpu.CompilerParams(vmem_limit_bytes=32 * 1024 * 1024),
        name="to_phi",
    )(gathered, origin, split_table(table), jnp.asarray(twist, jnp.float32))


def on_device(wigner, sky_alm, beam_blm, slot_col, slot_ell, order_of_column):
    cycles, orders, _ = wigner.shape
    degrees = order_of_column.shape[0]
    ells, blks = lax.axis_size("ell"), lax.axis_size("blk")
    sums = order_sums(wigner, sky_alm, beam_blm, slot_col, slot_ell, degrees // blks)
    gathered, origin = exchange(sums, order_of_column, orders, cycles)
    return to_phi(gathered, origin, cycles // ells, NPSI // blks, degrees)


def solution(mesh):
    return jax.shard_map(
        on_device,
        mesh=mesh,
        in_specs=(
            P(None, None, ("ell", "blk")),
            P(None, ("ell", "blk")),
            P(),
            P(("ell", "blk")),
            P(("ell", "blk")),
            P(),
        ),
        out_specs=P("ell", "blk", None),
        check_vma=False,
    )
```

time: 63.6 us -> 34.5 us (0.54)
  waiting for transfers between devices: 10.3 us -> 0 us
  starting transfers between devices: 9.28 us -> 0 us
  local copies, waits for them, and re-layouts: 7.98 us -> 0.01 us
  Pallas kernels: 27.4 us -> 34.3 us
  matrix products: 5.45 us -> 0 us
  other arithmetic: 2.61 us -> 0 us
    pallas_call x0 -> x2, Pallas kernels: none -> 15.8 us  [the longest x1 14.1 us: exchange(): pl.pallas_call(functools.partial(exchange_kernel, turns, lines), out_shap...]
    all_to_all x2 -> x0, waiting for transfers between devices: 10.3 us -> none  [the longest x1 6.07 us: on_device(): lax.all_to_all(partials, 'ell', split_axis=0, concat_axis=0, tiled=True)]
    all_to_all x2 -> x0, starting transfers between devices: 9.28 us -> none  [the longest x1 5.83 us: on_device(): lax.all_to_all(owned, 'blk', split_axis=2, concat_axis=3, tiled=True)]
    pallas_call x1, Pallas kernels: 27.4 us -> 18.5 us  [order_sums(): pl.pallas_call(functools.partial(sums_kernel, orders, cols, trips), out_s...]
    dot_general x5 -> x0, matrix products: 5.45 us -> none  [the longest x1 2.14 us: to_phi(): jnp.einsum('tpcj,cv->tpvj', weighted_im, select, precision=highest)]
    reshape x5 -> x0, local copies, waits for them, and re-layouts: 3.62 us -> none  [the longest x2 1.82 us: order_sums(): sky_alm.reshape(2, tiles, LANES).transpose(1, 0, 2)]
    unnamed x7 -> x8, local copies, waits for them, and re-layouts: 3.03 us -> 0.01 us
    cos x2 -> x0, other arithmetic: 2.19 us -> none  [the longest x1 2.04 us: to_phi(): cos_first = jnp.cos(angle)]
  transfers between devices with their start and end apart: 2 -> 0, of which waited for: 2 -> 0; matrix products, arithmetic and copies ran while one was open for 4% -> 0% of each run, Pallas kernels for 0% -> 0%
where the time goes in v2:
time: 34.5 us; the launch traced here: 34.3 us
  Pallas kernels  34.3 us (99%)
    pallas_call x1, Pallas kernels, order_sums(): pl.pallas_call(functools.partial(sums_kernel, orders, cols, trips), out_s...  18.5 us
    pallas_call x1, Pallas kernels, exchange(): pl.pallas_call(functools.partial(exchange_kernel, turns, lines), out_shap...  14.1 us
    pallas_call x1, Pallas kernels, to_phi(): pl.pallas_call(functools.partial(phi_kernel, gathered.shape[2] // 2), out...  1.72 us

profile of v2, /device:TPU:0, one launch (start us, length us, event | category | flops | bytes accessed | tf_op | source)
XLA Modules:
  0.0 34.3 jit_solution(3955135069328560505)
XLA Ops:
  0.0 0.0 copy-start.1
  0.0 0.0 copy-start
  0.0 0.0 copy-start.2
  0.0 0.0 copy-start.3
  0.0 18.5 %order_sums.1.sums_ref = f32[2,320,128]{2,1,0:T(8,128)S(1)} custom-call(bf16[17,8,65664]{2,1,0:T(8,128)(2,1)} %bitcast.6, f32[2,65664]{1,0:T(2,128)} %sky_hbm.1, s32[513,128]{1,0:T(8,128)} %bitcast.8, s32[513,128]{1,0:T(8,128)} %bitcast.9, f32[17,2,2048]{2,1,0:T(2,128)} %bitcast.7), custom_call_target="tpu_custom_call" | custom-call | tf_op jit(solution)/shard_map/order_sums/pallas_call | solution.py:291
  18.5 0.0 copy-done.1
  18.5 0.0 copy-done.3
  18.5 14.1 %exchange.1 = (f32[8,2,16,128]{3,2,1,0:T(8,128)S(1)}, s32[16,128]{1,0:T(8,128)S(1)}) custom-call(f32[2,320,128]{2,1,0:T(8,128)S(1)} %order_sums.1.sums_ref, bf16[2,128,80]{2,1,0:T(8,128)(2,1)S(1)} %copy-done.1, s32[1,2048]{1,0:T(1,128)S(1)} %bitcast.5), custom_call_target="tpu_custom_call" | custom-call | tf_op jit(solution)/shard_map/exchange/pallas_call | solution.py:436
  32.6 0.0 copy-done
  32.6 0.0 copy-done.2
  32.6 1.7 %to_phi.1 = f32[2,4,4096]{2,1,0:T(4,128)} custom-call(f32[8,2,16,128]{3,2,1,0:T(8,128)S(1)} %get-tuple-element.7.all_ref, s32[16,128]{1,0:T(8,128)S(1)} %get-tuple-element.8.from_ref, bf16[2,256,512]{2,1,0:T(8,128)(2,1)S(1)} %copy-done, f32[2,32,128]{2,1,0:T(8,128)S(1)} %copy-done.2), custom_call_target="tpu_custom_call" | custom-call | tf_op jit(solution)/shard_map/to_phi/pallas_call | solution.py:535
Async XLA Ops:
  0.0 18.5 %copy-start.1 = (bf16[2,128,80]{2,1,0:T(8,128)(2,1)S(1)}, bf16[2,128,80]{2,1,0:T(8,128)(2,1)}, u32[]{:S(2)}) copy-start(bf16[2,128,80]{2,1,0:T(8,128)(2,1)} %constant.15.table_ref) | copy-start | bytes 122884
  0.0 32.6 %copy-start = (bf16[2,256,512]{2,1,0:T(8,128)(2,1)S(1)}, bf16[2,256,512]{2,1,0:T(8,128)(2,1)}, u32[]{:S(2)}) copy-start(bf16[2,256,512]{2,1,0:T(8,128)(2,1)} %constant.22.table_ref) | copy-start | bytes 1572868
  0.0 32.6 %copy-start.2 = (f32[2,32,128]{2,1,0:T(8,128)S(1)}, f32[2,32,128]{2,1,0:T(8,128)}, u32[]{:S(2)}) copy-start(f32[2,32,128]{2,1,0:T(8,128)} %constant.8.clone.twist_ref) | copy-start | bytes 98308
  0.0 18.5 %copy-start.3 = (s32[2048]{0:T(1024)S(1)}, s32[2048]{0:T(1024)}, u32[]{:S(2)}) copy-start(s32[2048]{0:T(1024)} %param.14) | copy-start | bytes 24580
